TPU v7x, 32 devices: a whole 2x2x4 slice. The times are simulated.
32 devices in a mesh: aux: 4 (over z), orb: 8 (over y, x, core).
Axes of the slice: x: 2, y: 2, z: 4, core: 2. Of those that a mesh axis runs over, the one named last changes fastest.
Arguments:
- half: bfloat16 [64, 384, 3072], P('aux', 'orb'), may hold values from -1.25 to 1.25
- metric: bfloat16 [64, 64], P('aux'), may hold values from -1 to 2
- survive: int32 [4, 16, 24], P('aux', 'orb'), may hold values 0 or 1
Outputs:
- exchange_k: float32 [3072, 3072], P('orb', 'aux')
All inputs are finite; a program needn't handle non-finite values. No bound on the sum of `survive` on one device may be relied on, other than what follows from the above.
Results may differ from a plain program's by a relative error of at most 0.00098.
Values may be sent and summed in bfloat16 or wider, within the bound.
A program may use at most 128 MiB of HBM per device.

v0:
```python
import jax
import jax.numpy as jnp
from jax import lax
from jax.sharding import PartitionSpec as P


def shards(half, metric, survive):
    aux_local, occ_local, ao_count = half.shape
    blocks_aux, blocks_occ, blocks_ao = survive.shape
    gate = survive.astype(jnp.bfloat16)
    shaped = half.reshape(
        blocks_aux, aux_local, blocks_occ, occ_local // blocks_occ, blocks_ao, ao_count // blocks_ao
    )
    masked = (shaped * gate[:, None, :, None, :, None]).reshape(aux_local, occ_local, ao_count)
    portion = lax.all_gather(masked, "aux", axis=0, tiled=True)
    fit_total = jnp.dot(
        metric, portion.reshape(portion.shape[0], -1), preferred_element_type=jnp.float32
    )
    fitted = fit_total.astype(jnp.bfloat16).reshape(aux_local, occ_local, ao_count)
    group_width = ao_count // lax.axis_size("orb")
    row_start = lax.axis_index("orb") * group_width
    flat_rows = lax.all_gather(fitted, "orb", axis=1, tiled=True).reshape(-1, ao_count)
    left_rows = lax.dynamic_slice_in_dim(flat_rows, row_start, group_width, 1)
    partial_k = lax.dot_general(
        left_rows, flat_rows, (((0,), (0,)), ((), ())), preferred_element_type=jnp.float32
    )
    return lax.psum_scatter(partial_k, "aux", scatter_dimension=1, tiled=True)


def solution(mesh):
    return jax.shard_map(
        shards,
        mesh=mesh,
        in_specs=(P("aux", "orb", None), P("aux", None), P("aux", "orb", None)),
        out_specs=P("orb", "aux"),
        check_vma=False,
    )
```

profile of v0, /device:TPU:0, one launch (start us, length us, event | category | flops | bytes accessed | tf_op | source)
XLA Modules:
  0.0 656.1 jit_solution(17843219238067424248)
XLA Ops:
  6.5 0.0 copy-start
  6.5 0.0 all-gather.3.cloned.1.call-start
  6.5 0.7 convert_bitcast_fusion
  7.2 0.1 mul.21
  7.4 5.1 broadcast_multiply_fusion
  12.5 0.0 all-gather.3.cloned.1.call-update
  12.5 0.0 all-gather.5.cloned.1.call-start
  12.6 325.4 %all-gather.3.cloned.1.call-done = bf16[64,48,3072]{2,1,0:T(8,128)(2,1)} async-done(((bf16[16,48,3072]{2,1,0:T(8,128)(2,1)}), bf16[64,48,3072]{2,1,0:T(8,128)(2,1)}) %all-gather.3.cloned.1.call-update) | async-done | bytes 18874384 | tf_op jit(solution)/shard_map/all_gather | solution.py:15
  338.0 17.5 %copy.5 = bf16[8,8,48,3072]{3,1,2,0:T(8,128)(2,1)S(1)} copy(bf16[8,8,48,3072]{3,2,1,0:T(8,128)(2,1)} %bitcast.18) | data formatting | bytes 37748736
  355.5 0.0 copy-done
  355.5 2.7 convolution_convert_fusion
  358.3 4.7 copy.6
  363.0 0.0 all-gather.5.cloned.1.call-update
  363.0 0.0 reduce-scatter.2.cloned.1.call-start
  363.1 178.4 %all-gather.5.cloned.1.call-done = bf16[16,384,3072]{2,1,0:T(8,128)(2,1)} async-done(((bf16[16,48,3072]{2,1,0:T(8,128)(2,1)}), bf16[16,384,3072]{2,1,0:T(8,128)(2,1)}) %all-gather.5.cloned.1.call-update) | async-done | bytes 37748752 | tf_op jit(solution)/shard_map/all_gather | solution.py:22
  541.5 0.0 copy-start.1
  541.5 22.4 %fusion = f32[384,3072]{1,0:T(8,128)} fusion(bf16[6144,3072]{1,0:T(8,128)(2,1)} %bitcast.22, s32[]{:T(128)S(6)} %select_n.3), kind=kOutput, calls=%fused_computation.1 | convolution fusion | flops 14495514624 | bytes 47185924 | tf_op jit(solution)/shard_map/dot_general | solution.py:24
  563.9 0.0 reduce-scatter.2.cloned.1.call-update
  563.9 85.6 %reduce-scatter.2.cloned.1.call-done = f32[384,768]{1,0:T(8,128)} async-done(((f32[384,3072]{1,0:T(8,128)}), f32[384,768]{1,0:T(8,128)}) %reduce-scatter.2.cloned.1.call-update) | async-done | bytes 1179664 | tf_op jit(solution)/shard_map/reduce_scatter | solution.py:27
  649.5 0.0 copy-done.1
  (1 shorter events, 0.0 us)
Async XLA Ops:
  6.5 349.0 %copy-start = (bf16[16,64]{1,0:T(8,128)(2,1)S(1)}, bf16[16,64]{1,0:T(8,128)(2,1)}, u32[]{:S(2)}) copy-start(bf16[16,64]{1,0:T(8,128)(2,1)} %param.4) | copy-start | bytes 6148
  6.5 331.5 %all-gather.3.cloned.1.call-start = ((), (), s32[]{:S(2)}) async-start(), calls=%async_computation.1 | async-start | bytes 23592960 | tf_op jit(solution)/shard_map/all_gather | solution.py:15
  12.5 528.9 %all-gather.5.cloned.1.call-start = ((), (), s32[]{:S(2)}) async-start(), calls=%async_computation.2 | async-start | bytes 42467328 | tf_op jit(solution)/shard_map/all_gather | solution.py:22
  363.0 286.5 %reduce-scatter.2.cloned.1.call-start = ((), (), s32[]{:S(2)}) async-start(), calls=%async_computation.3 | async-start | bytes 5898240 | tf_op jit(solution)/shard_map/reduce_scatter | solution.py:27
  541.5 108.1 %copy-start.1 = (bf16[16,64]{1,0:T(8,128)(2,1)S(1)}, bf16[16,64]{1,0:T(8,128)(2,1)}, u32[]{:S(2)}) copy-start(bf16[16,64]{1,0:T(8,128)(2,1)} %param.4) | copy-start | bytes 6148
Sparse Core Ops, SparseCore 0:
  12.7 325.2 all-gather.2
  363.2 178.2 all-gather.4
  564.0 85.4 reduce-scatter.1
where the time goes:
time: 656 us
  waiting for transfers between devices  589 us (90%)
  matrix products  25.2 us (4%)
  local copies, waits for them, and re-layouts  22.4 us (3%)
  between operations  13.2 us (2%)
    all_gather x1, waiting for transfers between devices, shards(): portion = lax.all_gather(masked, 'aux', axis=0, tiled=True)  325 us
    all_gather x1, waiting for transfers between devices, shards(): lax.all_gather(fitted, 'orb', axis=1, tiled=True).reshape(-1, ao_count)  178 us
    reduce_scatter x1, waiting for transfers between devices, shards(): return lax.psum_scatter(partial_k, 'aux', scatter_dimension=1, tiled=True)  85.6 us
    dot_general x1, matrix products, shards(): lax.dot_general(left_rows, flat_rows, (((0,), (0,)), ((), ())), preferred...  22.4 us
    unnamed x7, local copies, waits for them, and re-layouts  22.3 us
  transfers between devices with their start and end apart: 3, of which 3 were waited for; matrix products, arithmetic and copies ran while one was open for 0% of the time, Pallas kernels for 0%

commit v1 on v0

v1 whole, which is shorter than its diff:
```python
import functools

import jax
import jax.numpy as jnp
from jax import lax
from jax.experimental import pallas as pl
from jax.experimental.pallas import tpu as pltpu
from jax.sharding import PartitionSpec as P

MESH = pl.DeviceIdType.MESH
F32 = jnp.float32


def gated(half, survive):
    aux_local, occ_local, ao_count = half.shape
    blocks_aux, blocks_occ, blocks_ao = survive.shape
    gate = survive.astype(jnp.bfloat16)
    shaped = half.reshape(
        blocks_aux, aux_local, blocks_occ, occ_local // blocks_occ, blocks_ao, ao_count // blocks_ao
    )
    return (shaped * gate[:, None, :, None, :, None]).reshape(aux_local, occ_local, ao_count)


def plain(half, metric, survive):
    aux_local, occ_local, ao_count = half.shape
    portion = lax.all_gather(gated(half, survive), "aux", axis=0, tiled=True)
    fit_total = jnp.dot(metric, portion.reshape(portion.shape[0], -1), preferred_element_type=F32)
    fitted = fit_total.astype(jnp.bfloat16).reshape(aux_local, occ_local, ao_count)
    group_width = ao_count // lax.axis_size("orb")
    row_start = lax.axis_index("orb") * group_width
    flat_rows = lax.all_gather(fitted, "orb", axis=1, tiled=True).reshape(-1, ao_count)
    left_rows = lax.dynamic_slice_in_dim(flat_rows, row_start, group_width, 1)
    partial_k = lax.dot_general(
        left_rows, flat_rows, (((0,), (0,)), ((), ())), preferred_element_type=F32
    )
    return lax.psum_scatter(partial_k, "aux", scatter_dimension=1, tiled=True)


def kernel(
    m_ref, kron_ref, out_ref, held, fit, left, acc, peer, tile, via, last,
    zs, zr, xs, xr, ys, yr, fs, fr, ps, pr, rs, rr,
):
    z = lax.axis_index("aux")
    orb = lax.axis_index("orb")
    n_aux = m_ref.shape[0]
    unit = m_ref.shape[1]
    ao = m_ref.shape[2]
    chip = orb // 2
    core = orb % 2
    pair_rows = acc.shape[0]
    rows = pair_rows // 2
    cols = out_ref.shape[1]
    half_rows = rows // 2
    x_peer = orb + 2 - 4 * (chip % 2)
    y_peer = orb + 4 - 8 * (chip // 2)
    partner = orb + 1 - 2 * core
    up, down, far = (z + 1) % n_aux, (z + n_aux - 1) % n_aux, (z + 2) % n_aux

    barrier = pltpu.get_barrier_semaphore()
    for a in (up, down, far):
        pl.semaphore_signal(barrier, inc=1, device_id={"aux": a, "orb": orb}, device_id_type=MESH)
    for o in (x_peer, y_peer, partner):
        pl.semaphore_signal(barrier, inc=1, device_id={"aux": z, "orb": o}, device_id_type=MESH)
    pl.semaphore_wait(barrier, 6)

    def remote(src, dst, send, recv, a, o):
        return pltpu.make_async_remote_copy(
            src_ref=src, dst_ref=dst, send_sem=send, recv_sem=recv,
            device_id={"aux": a, "orb": o}, device_id_type=MESH,
        )

    def span(s):
        return pl.ds(pl.multiple_of(s * unit, unit), unit)

    def source(d):
        return (z + n_aux - d) % n_aux

    spread = {}
    for d in (1, 3, 2):
        there = (z + d) % n_aux
        spread[d] = remote(m_ref.at[there], held.at[0, span(z)], zs.at[d], zr.at[d], there, orb)
        spread[d].start()

    to_x, to_y, onward = {}, {}, {}

    def share(d):
        own = span(source(d))
        if d:
            spread[d].wait_recv()
        block = held.at[0, own] if d else m_ref.at[z]
        to_x[d] = remote(block, held.at[1, own], xs.at[d], xr.at[d], z, x_peer)
        to_y[d] = remote(block, held.at[2, own], ys.at[d], yr.at[d], z, y_peer)
        to_x[d].start()
        to_y[d].start()

    def forward(d, from_x):
        own = span(source(d))
        if from_x:
            to_x[d].wait_recv()
            onward[d] = remote(held.at[1, own], held.at[3, own], fs.at[d], fr.at[d], z, y_peer)
        else:
            to_y[d].wait_recv()
            onward[d] = remote(held.at[2, own], held.at[3, own], fs.at[d], fr.at[d], z, x_peer)
        onward[d].start()

    step = 512
    mine = pl.ds(pl.multiple_of(chip * pair_rows, pair_rows), pair_rows)

    def contract(slot, first):
        @pl.loop(0, ao // step)
        def _(t):
            at = pl.ds(pl.multiple_of(t * step, step), step)
            fit[:, at] = jnp.dot(
                kron_ref[...], held[slot, :, at], preferred_element_type=F32
            ).astype(fit.dtype)

        left[...] = fit[:, mine].T

        @pl.loop(0, ao // step)
        def _(t):
            at = pl.ds(pl.multiple_of(t * step, step), step)
            more = jnp.dot(left[...], fit[:, at], preferred_element_type=F32)
            acc[:, at] = more if first else acc[:, at] + more

    share(0)
    held[0, span(z), :] = m_ref[z]
    share(1)
    share(3)
    forward(0, True)
    share(2)
    forward(1, False)
    contract(0, True)
    forward(3, True)
    to_x[1].wait_recv()
    to_x[2].wait_recv()
    contract(1, False)
    forward(2, False)
    to_y[0].wait_recv()
    to_y[3].wait_recv()
    contract(2, False)
    for d in range(4):
        onward[d].wait_recv()
    contract(3, False)

    def across(a):
        return pl.ds(pl.multiple_of(a * cols, cols), cols)

    my_rows = pl.ds(pl.multiple_of(core * rows, rows), rows)
    other_rows = pl.ds(pl.multiple_of((1 - core) * rows, rows), rows)
    order = (far, up, down, z)
    swaps = []
    for n, a in enumerate(order):
        swap = remote(acc.at[other_rows, across(a)], peer.at[n], ps.at[n], pr.at[n], z, partner)
        swap.start()
        swaps.append(swap)

    low, high = pl.ds(0, half_rows), pl.ds(half_rows, half_rows)

    def settle(n):
        swaps[n].wait_recv()
        tile[n] = acc[my_rows, across(order[n])] + peer[n]

    settle(0)
    far_up = remote(tile.at[0, low], via.at[0], rs.at[0], rr.at[0], up, orb)
    far_down = remote(tile.at[0, high], via.at[1], rs.at[1], rr.at[1], down, orb)
    far_up.start()
    far_down.start()
    settle(1)
    near_up = remote(tile.at[1, high], last.at[0, high], rs.at[2], rr.at[2], up, orb)
    near_up.start()
    settle(2)
    near_down = remote(tile.at[2, low], last.at[1, low], rs.at[3], rr.at[3], down, orb)
    near_down.start()
    settle(3)
    far_up.wait_recv()
    tile[1, low] += via[0]
    sum_up = remote(tile.at[1, low], last.at[0, low], rs.at[4], rr.at[4], up, orb)
    sum_up.start()
    far_down.wait_recv()
    tile[2, high] += via[1]
    sum_down = remote(tile.at[2, high], last.at[1, high], rs.at[5], rr.at[5], down, orb)
    sum_down.start()
    for copy in (near_up, near_down, sum_up, sum_down):
        copy.wait_recv()
    out_ref[...] = tile[3] + last[0] + last[1]
    for copy in (
        *spread.values(), *to_x.values(), *to_y.values(), *onward.values(), *swaps,
        far_up, far_down, near_up, near_down, sum_up, sum_down,
    ):
        copy.wait_send()


def direct(half, metric, survive):
    aux_local, occ_local, ao = half.shape
    n_aux, n_orb = lax.axis_size("aux"), lax.axis_size("orb")
    part = occ_local // n_aux
    blocks = gated(half, survive).reshape(aux_local, n_aux, part, ao)
    blocks = blocks.transpose(1, 0, 2, 3).reshape(n_aux, aux_local * part, ao)
    whole_metric = lax.all_gather(metric, "aux", axis=0, tiled=True)
    kron = jnp.kron(whole_metric, jnp.eye(part, dtype=metric.dtype))
    depth = kron.shape[0]
    rows, cols = ao // n_orb, ao // n_aux
    dma = pltpu.SemaphoreType.DMA
    bf16 = jnp.bfloat16
    return pl.pallas_call(
        kernel,
        out_shape=jax.ShapeDtypeStruct((rows, cols), F32),
        in_specs=[pl.BlockSpec(memory_space=pltpu.VMEM)] * 2,
        out_specs=pl.BlockSpec(memory_space=pltpu.VMEM),
        scratch_shapes=[
            pltpu.VMEM((4, depth, ao), bf16),
            pltpu.VMEM((depth, ao), bf16),
            pltpu.VMEM((2 * rows, depth), bf16),
            pltpu.VMEM((2 * rows, ao), F32),
            pltpu.VMEM((4, rows, cols), F32),
            pltpu.VMEM((4, rows, cols), F32),
            pltpu.VMEM((2, rows // 2, cols), F32),
            pltpu.VMEM((2, rows, cols), F32),
        ]
        + [dma((4,))] * 10
        + [dma((6,))] * 2,
        compiler_params=pltpu.CompilerParams(
            collective_id=0, has_side_effects=True, vmem_limit_bytes=66 * 1000 * 1000
        ),
    )(blocks, kron)


def solution(mesh):
    square = mesh.shape["aux"] == 4 and mesh.shape["orb"] == 8
    return jax.shard_map(
        direct if square else plain,
        mesh=mesh,
        in_specs=(P("aux", "orb", None), P("aux", None), P("aux", "orb", None)),
        out_specs=P("orb", "aux"),
        check_vma=False,
    )
```

time: 656 us -> 331 us (0.50)
  waiting for transfers between devices: 589 us -> 0 us
  Pallas kernels: 0 us -> 267 us
  matrix products: 25.2 us -> 0 us
  local copies, waits for them, and re-layouts: 22.4 us -> 38.8 us
  blocking collectives: 0 us -> 15 us
  between operations: 13.2 us -> 0.04 us
    all_gather x2 -> x0, waiting for transfers between devices: 504 us -> none  [the longest x1 325 us: shards(): portion = lax.all_gather(masked, 'aux', axis=0, tiled=True)]
    pallas_call x0 -> x1, Pallas kernels: none -> 267 us  [direct(): pl.pallas_call(kernel, out_shape=jax.ShapeDtypeStruct((rows, cols), F32),...]
    reduce_scatter x1 -> x0, waiting for transfers between devices: 85.6 us -> none  [shards(): return lax.psum_scatter(partial_k, 'aux', scatter_dimension=1, tiled=True)]
    dot_general x2 -> x0, matrix products: 25.2 us -> none  [the longest x1 22.4 us: shards(): lax.dot_general(left_rows, flat_rows, (((0,), (0,)), ((), ())), preferred...]
    mul x1 -> x2, local copies, waits for them, and re-layouts: 0.11 us -> 24.3 us  [the longest x1 24.2 us: direct(): kron = jnp.kron(whole_metric, jnp.eye(part, dtype=metric.dtype))]
    all_gather x0 -> x1, blocking collectives: none -> 15 us  [direct(): whole_metric = lax.all_gather(metric, 'aux', axis=0, tiled=True)]
    unnamed x7 -> x3, local copies, waits for them, and re-layouts: 22.3 us -> 7.3 us
  transfers between devices with their start and end apart: 3 -> 0, of which waited for: 3 -> 0; matrix products, arithmetic and copies ran while one was open for 0% -> 0% of each run, Pallas kernels for 0% -> 0%
where the time goes in v1:
time: 331 us; the launch traced here: 328 us
  Pallas kernels  267 us (81%)
  local copies, waits for them, and re-layouts  38.8 us (12%)
  blocking collectives  15 us (5%)
  other arithmetic  6.73 us (2%)
    pallas_call x1, Pallas kernels, direct(): pl.pallas_call(kernel, out_shape=jax.ShapeDtypeStruct((rows, cols), F32),...  267 us
    mul x1, local copies, waits for them, and re-layouts, direct(): kron = jnp.kron(whole_metric, jnp.eye(part, dtype=metric.dtype))  24.2 us
    all_gather x1, blocking collectives, direct(): whole_metric = lax.all_gather(metric, 'aux', axis=0, tiled=True)  15 us
    unnamed x3, local copies, waits for them, and re-layouts  7.3 us

profile of v1, /device:TPU:0, one launch (start us, length us, event | category | flops | bytes accessed | tf_op | source)
XLA Modules:
  0.0 327.8 jit_solution(1204093327627624489)
XLA Ops:
  0.0 0.7 convert_bitcast_fusion
  0.7 15.0 %all_gather.3 = bf16[64,64]{1,0:T(8,128)(2,1)S(1)} all-gather(bf16[16,64]{1,0:T(8,128)(2,1)} %param.4), channel_id=1, replica_groups=mesh['aux'=4,'orb'=8] {'aux'}, dimensions={0}, use_global_device_ids=true | all-gather | bytes 10240 | tf_op jit(solution)/shard_map/all_gather | solution.py:199
  15.7 0.1 mul.42
  15.8 4.9 %copy.5 = bf16[16,48,3072]{2,0,1:T(8,128)(2,1)S(1)} copy(bf16[16,48,3072]{2,1,0:T(8,128)(2,1)} %param.3) | data formatting | bytes 9437184 | tf_op args[0]
  20.7 0.3 multiply_bitcast_fusion
  21.1 3.6 %copy.6 = bf16[4,16,12,3072]{3,0,2,1:T(4,128)(2,1)S(1)} copy(bf16[4,16,12,3072]{3,1,2,0:T(8,128)(2,1)S(1)} %multiply_bitcast_fusion) | data formatting | bytes 9437184 | tf_op jit(solution)/shard_map/transpose | solution.py:198
  24.7 3.5 %copy.7.m_ref = bf16[4,192,3072]{2,1,0:T(8,128)(2,1)} copy(bf16[4,192,3072]{2,0,1:T(4,128)(2,1)S(1)} %bitcast.13) | data formatting | bytes 9437184 | tf_op jit(solution)/shard_map/reshape | solution.py:198
  28.2 5.7 %broadcast_multiply_fusion = bf16[64,12,64,12]{3,2,1,0:T(8,128)(2,1)} fusion(bf16[12,12]{1,0:T(8,128)(2,1)S(1)} %fusion, bf16[64,64]{1,0:T(8,128)(2,1)S(1)} %all_gather.3), kind=kLoop, calls=%fused_computation | loop fusion | flops 589824 | bytes 1188128 | tf_op jit(solution)/shard_map/jit(kron)/mul | solution.py:200
  33.9 24.2 %mul.49.kron_ref = bf16[768,768]{1,0:T(8,128)(2,1)} reshape(bf16[64,12,64,12]{3,2,1,0:T(8,128)(2,1)} %broadcast_multiply_fusion) | data formatting | bytes 2359296 | tf_op jit(solution)/shard_map/jit(kron)/mul | solution.py:200
  58.2 267.2 %shard_map.37 = f32[384,768]{1,0:T(8,128)} custom-call(bf16[4,192,3072]{2,1,0:T(8,128)(2,1)} %copy.7.m_ref, bf16[768,768]{1,0:T(8,128)(2,1)} %mul.49.kron_ref), custom_call_target="tpu_custom_call" | custom-call | tf_op jit(solution)/shard_map/pallas_call | solution.py:205
  325.4 2.4 copy.12
  (2 shorter events, 0.0 us)

commit v2 on v1

--- a/solution.py
+++ b/solution.py
@@ -37,8 +37,8 @@
 
 
 def kernel(
-    m_ref, kron_ref, out_ref, held, fit, left, acc, peer, tile, via, last,
-    zs, zr, xs, xr, ys, yr, fs, fr, ps, pr, rs, rr,
+    aux_local, m_ref, metric_ref, out_ref, held, fit, left, acc, peer, tile, via, last, whole, kron_ref,
+    gs, gr, zs, zr, xs, xr, ys, yr, fs, fr, ps, pr, rs, rr,
 ):
     z = lax.axis_index("aux")
     orb = lax.axis_index("orb")
@@ -75,6 +75,12 @@
     def source(d):
         return (z + n_aux - d) % n_aux
 
+    metric_rows = pl.ds(pl.multiple_of(z * aux_local, aux_local), aux_local)
+    gather = []
+    for d in (1, 3, 2):
+        copy = remote(metric_ref, whole.at[metric_rows], gs.at[d], gr.at[d], (z + d) % n_aux, orb)
+        copy.start()
+        gather.append(copy)
     spread = {}
     for d in (1, 3, 2):
         there = (z + d) % n_aux
@@ -122,8 +128,33 @@
             more = jnp.dot(left[...], fit[:, at], preferred_element_type=F32)
             acc[:, at] = more if first else acc[:, at] + more
 
+    def build_kron():
+        whole[metric_rows, :] = metric_ref[...]
+        for copy in gather:
+            copy.wait_recv()
+        depth, width = kron_ref.shape[0], whole.shape[1]
+
+        def aux_of(r):
+            return lax.div(r, unit) * aux_local + lax.rem(r, aux_local)
+
+        def orbital_of(r):
+            return lax.div(lax.rem(r, unit), aux_local)
+
+        i32, bf16 = jnp.int32, kron_ref.dtype
+        by_row = aux_of(lax.broadcasted_iota(i32, (width, depth), 1))
+        pick = jnp.where(by_row == lax.broadcasted_iota(i32, (width, depth), 0), 1.0, 0.0)
+        spread_cols = jnp.dot(whole[...], pick.astype(bf16), preferred_element_type=F32).astype(bf16)
+        by_col = aux_of(lax.broadcasted_iota(i32, (depth, whole.shape[0]), 0))
+        take = jnp.where(by_col == lax.broadcasted_iota(i32, (depth, whole.shape[0]), 1), 1.0, 0.0)
+        both = jnp.dot(take.astype(bf16), spread_cols, preferred_element_type=F32)
+        same = orbital_of(lax.broadcasted_iota(i32, (depth, depth), 0)) == orbital_of(
+            lax.broadcasted_iota(i32, (depth, depth), 1)
+        )
+        kron_ref[...] = jnp.where(same, both, 0.0).astype(bf16)
+
     share(0)
     held[0, span(z), :] = m_ref[z]
+    build_kron()
     share(1)
     share(3)
     forward(0, True)
@@ -184,7 +215,7 @@
         copy.wait_recv()
     out_ref[...] = tile[3] + last[0] + last[1]
     for copy in (
-        *spread.values(), *to_x.values(), *to_y.values(), *onward.values(), *swaps,
+        *gather, *spread.values(), *to_x.values(), *to_y.values(), *onward.values(), *swaps,
         far_up, far_down, near_up, near_down, sum_up, sum_down,
     ):
         copy.wait_send()
@@ -194,16 +225,16 @@
     aux_local, occ_local, ao = half.shape
     n_aux, n_orb = lax.axis_size("aux"), lax.axis_size("orb")
     part = occ_local // n_aux
-    blocks = gated(half, survive).reshape(aux_local, n_aux, part, ao)
-    blocks = blocks.transpose(1, 0, 2, 3).reshape(n_aux, aux_local * part, ao)
-    whole_metric = lax.all_gather(metric, "aux", axis=0, tiled=True)
-    kron = jnp.kron(whole_metric, jnp.eye(part, dtype=metric.dtype))
-    depth = kron.shape[0]
+    blocks = gated(half, survive).transpose(1, 0, 2).reshape(n_aux, part * aux_local, ao)
+    n_fit = n_aux * aux_local
+    width = -(-n_fit // 128) * 128
+    metric = jnp.pad(metric, ((0, 0), (0, width - n_fit)))
+    depth = n_fit * part
     rows, cols = ao // n_orb, ao // n_aux
     dma = pltpu.SemaphoreType.DMA
     bf16 = jnp.bfloat16
     return pl.pallas_call(
-        kernel,
+        functools.partial(kernel, aux_local),
         out_shape=jax.ShapeDtypeStruct((rows, cols), F32),
         in_specs=[pl.BlockSpec(memory_space=pltpu.VMEM)] * 2,
         out_specs=pl.BlockSpec(memory_space=pltpu.VMEM),
@@ -216,13 +247,15 @@
             pltpu.VMEM((4, rows, cols), F32),
             pltpu.VMEM((2, rows // 2, cols), F32),
             pltpu.VMEM((2, rows, cols), F32),
+            pltpu.VMEM((n_fit, width), bf16),
+            pltpu.VMEM((depth, depth), bf16),
         ]
-        + [dma((4,))] * 10
+        + [dma((4,))] * 12
         + [dma((6,))] * 2,
         compiler_params=pltpu.CompilerParams(
             collective_id=0, has_side_effects=True, vmem_limit_bytes=66 * 1000 * 1000
         ),
-    )(blocks, kron)
+    )(blocks, metric)
 
 
 def solution(mesh):

time: 331 us -> 288 us (0.87)
  local copies, waits for them, and re-layouts: 38.8 us -> 7.82 us
  blocking collectives: 15 us -> 0 us
  Pallas kernels: 267 us -> 275 us
    mul x1 -> x0, local copies, waits for them, and re-layouts: 24.2 us -> none  [direct(): kron = jnp.kron(whole_metric, jnp.eye(part, dtype=metric.dtype))]
    all_gather x1 -> x0, blocking collectives: 15 us -> none  [direct(): whole_metric = lax.all_gather(metric, 'aux', axis=0, tiled=True)]
    pallas_call x1, Pallas kernels: 267 us -> 275 us  [direct(): pl.pallas_call(functools.partial(kernel, aux_local), out_shape=jax.ShapeD...]
    mul x1 -> x0, other arithmetic: 5.72 us -> none  [direct(): kron = jnp.kron(whole_metric, jnp.eye(part, dtype=metric.dtype))]
    unnamed x3 -> x4, local copies, waits for them, and re-layouts: 7.3 us -> 2.41 us
    reshape x1 -> x0, local copies, waits for them, and re-layouts: 3.49 us -> none  [direct(): blocks = blocks.transpose(1, 0, 2, 3).reshape(n_aux, aux_local * part, ao)]
where the time goes in v2:
time: 288 us; the launch traced here: 286 us
  Pallas kernels  275 us (95%)
  local copies, waits for them, and re-layouts  7.82 us (3%)
  other arithmetic  3.48 us (1%)
    pallas_call x1, Pallas kernels, direct(): pl.pallas_call(functools.partial(kernel, aux_local), out_shape=jax.ShapeD...  275 us

profile of v2, /device:TPU:0, one launch (start us, length us, event | category | flops | bytes accessed | tf_op | source)
XLA Modules:
  0.0 286.3 jit_solution(13193111221086492569)
XLA Ops:
  0.0 0.7 convert_bitcast_fusion
  0.7 0.1 mul.18
  0.8 2.8 multiply_bitcast_fusion
  3.7 0.0 copy-start
  3.7 4.7 %copy.4 = bf16[48,16,3072]{2,1,0:T(8,128)(2,1)} copy(bf16[48,16,3072]{2,0,1:T(8,128)(2,1)S(1)} %multiply_bitcast_fusion) | data formatting | bytes 9437184 | tf_op jit(solution)/shard_map/transpose | solution.py:228
  8.4 0.0 copy-done
  8.4 0.6 pad.4.metric_ref
  9.0 274.9 %shard_map.37 = f32[384,768]{1,0:T(8,128)} custom-call(bf16[4,192,3072]{2,1,0:T(8,128)(2,1)} %bitcast.10, bf16[16,128]{1,0:T(8,128)(2,1)} %pad.4.metric_ref), custom_call_target="tpu_custom_call" | custom-call | tf_op jit(solution)/shard_map/pallas_call | solution.py:236
  283.9 2.4 copy.9
  (1 shorter events, 0.0 us)
Async XLA Ops:
  3.7 4.7 %copy-start = (bf16[16,64]{1,0:T(8,128)(2,1)S(1)}, bf16[16,64]{1,0:T(8,128)(2,1)}, u32[]{:S(2)}) copy-start(bf16[16,64]{1,0:T(8,128)(2,1)} %param.4) | copy-start | bytes 6148
